TPU v7x, 32 devices: a whole 2x2x4 slice. The times are simulated.
32 devices in a mesh: dp: 8 (over z, x), seq: 4 (over y, core).
Axes of the slice: x: 2, y: 2, z: 4, core: 2. Of those that a mesh axis runs over, the one named last changes fastest.
Arguments:
- queries: bfloat16 [4096, 2048], P(('dp', 'seq')), may hold values from -6 to 6
- keys: bfloat16 [4096, 2048], P(('dp', 'seq')), may hold values from -6 to 6
- values: bfloat16 [4096, 2048], P(('dp', 'seq')), may hold values from -6 to 6
- q_gain: float32 [2048], replicated, may hold values from 0.25 to 1.75
- k_gain: float32 [2048], replicated, may hold values from 0.25 to 1.75
- out_grad: bfloat16 [4096, 2048], P(('dp', 'seq')), may hold values from -16 to 16
- segments: int32 [8, 512], P('dp'), may hold values from 0 to 3, never falling along the last dimension, each value on 1 to 256 neighbouring positions
- visible: int32 [8, 512], P('dp'), may hold values 0 or 1
Outputs:
- attn_out: bfloat16 [4096, 2048], P(('dp', 'seq'))
- query_grad: bfloat16 [4096, 2048], P(('dp', 'seq'))
- key_grad: bfloat16 [4096, 2048], P(('dp', 'seq'))
- value_grad: bfloat16 [4096, 2048], P(('dp', 'seq'))
- q_gain_grad: float32 [2048], replicated
- k_gain_grad: float32 [2048], replicated
Inputs may be any that keep to these rules, and one draw needn't show every extreme that they name: `segments`: along each packed sequence the clip numbers never fall; each of the 4 clips holds 1 to 256 slots.
All inputs are finite; a program needn't handle non-finite values. No bound on the sum of `visible` on one device may be relied on, other than what follows from the above.
Results may differ from a plain program's by a relative error of at most 0.012.
The roundings to bfloat16 on the way count: a program that leaves them out, or rounds other values in their place, can miss the bound.
Values may be sent and summed in bfloat16 or wider, within the bound.
No kernel may reach another device: no remote copies, remote signals or barrier semaphores. Data moves between devices by JAX's collectives and lax.ppermute only.
A program may use at most 64 MiB of HBM per device.

v0:
```python
import jax
import jax.numpy as jnp
from jax import lax
from jax.sharding import PartitionSpec as P

D_HEAD = 128
epsilon = 1e-06


def normalize(raw_rows, gain_vec):
    raw_f32 = raw_rows.astype(jnp.float32)
    inv_rms = lax.rsqrt(jnp.mean(raw_f32 * raw_f32, axis=-1, keepdims=True) + epsilon)
    return ((raw_f32 * inv_rms * gain_vec).astype(jnp.bfloat16), inv_rms)


def norm_back(raw_rows, inv_rms, gain_vec, grad_norm):
    raw_f32 = raw_rows.astype(jnp.float32)
    grad_f32 = grad_norm.astype(jnp.float32)
    scaled_grad = gain_vec * grad_f32
    mean_term = jnp.mean(scaled_grad * raw_f32, axis=-1, keepdims=True)
    grad_raw = inv_rms * scaled_grad - raw_f32 * inv_rms**3 * mean_term
    return (grad_raw.astype(jnp.bfloat16), jnp.sum(grad_f32 * raw_f32 * inv_rms, axis=0))


def attend(q_norm, k_norm, val_rows, grad_rows, seg_row, vis_row, keep_out):
    seq_rows, feature_count = q_norm.shape
    head_count = feature_count // D_HEAD
    score_scale = D_HEAD ** (-0.5)
    block_rows = 512
    block_count = seq_rows // block_rows
    k_three = k_norm.reshape(seq_rows, head_count, D_HEAD)
    v_three = val_rows.reshape(seq_rows, head_count, D_HEAD)
    positions = jnp.arange(seq_rows, dtype=jnp.int32)
    key_open = vis_row == 1

    def one_block(totals, block_index):
        block_start = block_index * block_rows
        q_block = lax.dynamic_slice_in_dim(q_norm, block_start, block_rows, 0).reshape(
            block_rows, head_count, D_HEAD
        )
        seg_block = lax.dynamic_slice_in_dim(seg_row, block_start, block_rows, 0)
        pos_block = block_start + jnp.arange(block_rows, dtype=jnp.int32)
        allowed = (seg_block[:, None] == seg_row[None, :]) & (
            key_open[None, :] | (pos_block[:, None] == positions[None, :])
        )
        scores = (
            jnp.einsum("shd,thd->hst", q_block, k_three, preferred_element_type=jnp.float32)
            * score_scale
        )
        scores = jnp.where(allowed[None], scores, -1e30)
        row_max = jnp.max(scores, axis=-1, keepdims=True)
        weights = jnp.exp(scores - row_max)
        attn_prob = weights / jnp.sum(weights, axis=-1, keepdims=True)
        prob_half = attn_prob.astype(jnp.bfloat16)
        block_out = jnp.zeros((block_rows, feature_count), jnp.bfloat16)
        if keep_out:
            block_out = (
                jnp.einsum("hst,thd->shd", prob_half, v_three, preferred_element_type=jnp.float32)
                .reshape(block_rows, feature_count)
                .astype(jnp.bfloat16)
            )
        if grad_rows is None:
            return (totals, (block_out, block_out))
        grad_block = lax.dynamic_slice_in_dim(grad_rows, block_start, block_rows, 0).reshape(
            block_rows, head_count, D_HEAD
        )
        dprob = jnp.einsum("shd,thd->hst", grad_block, v_three, preferred_element_type=jnp.float32)
        value_add = jnp.einsum(
            "hst,shd->thd", prob_half, grad_block, preferred_element_type=jnp.float32
        )
        row_dot = jnp.sum(attn_prob * dprob, axis=-1, keepdims=True)
        score_grad = (attn_prob * (dprob - row_dot) * score_scale).astype(jnp.bfloat16)
        q_grad = (
            jnp.einsum("hst,thd->shd", score_grad, k_three, preferred_element_type=jnp.float32)
            .reshape(block_rows, feature_count)
            .astype(jnp.bfloat16)
        )
        key_add = jnp.einsum(
            "hst,shd->thd", score_grad, q_block, preferred_element_type=jnp.float32
        )
        return ((totals[0] + key_add, totals[1] + value_add), (block_out, q_grad))

    empty = jnp.zeros((seq_rows, head_count, D_HEAD), jnp.float32)
    totals, stacked = lax.scan(one_block, (empty, empty), jnp.arange(block_count, dtype=jnp.int32))
    attn_out = stacked[0].reshape(seq_rows, feature_count)
    if grad_rows is None:
        return attn_out
    q_grad = stacked[1].reshape(seq_rows, feature_count)
    k_grad = totals[0].reshape(seq_rows, feature_count).astype(jnp.bfloat16)
    v_grad = totals[1].reshape(seq_rows, feature_count).astype(jnp.bfloat16)
    return (attn_out, q_grad, k_grad, v_grad)


def per_device(queries, keys, values, q_gain, k_gain, out_grad, segments, visible):
    q_norm, q_inv = normalize(queries, q_gain)
    k_norm, k_inv = normalize(keys, k_gain)
    seg_row = segments[0]
    vis_row = visible[0]
    query_heads, key_heads, value_heads = (
        lax.all_to_all(q_norm, "seq", split_axis=1, concat_axis=0, tiled=True),
        lax.all_to_all(k_norm, "seq", split_axis=1, concat_axis=0, tiled=True),
        lax.all_to_all(values, "seq", split_axis=1, concat_axis=0, tiled=True),
    )
    out_part = attend(query_heads, key_heads, value_heads, None, seg_row, vis_row, True)
    attn_out = lax.all_to_all(out_part, "seq", split_axis=0, concat_axis=1, tiled=True)
    grad_heads = lax.all_to_all(out_grad, "seq", split_axis=1, concat_axis=0, tiled=True)
    unused_out, q_part, k_part, v_part = attend(
        query_heads, key_heads, value_heads, grad_heads, seg_row, vis_row, False
    )
    q_grad, k_grad, value_grad = (
        lax.all_to_all(q_part, "seq", split_axis=0, concat_axis=1, tiled=True),
        lax.all_to_all(k_part, "seq", split_axis=0, concat_axis=1, tiled=True),
        lax.all_to_all(v_part, "seq", split_axis=0, concat_axis=1, tiled=True),
    )
    query_grad, q_gain_part = norm_back(queries, q_inv, q_gain, q_grad)
    key_grad, k_gain_part = norm_back(keys, k_inv, k_gain, k_grad)
    q_gain_grad, k_gain_grad = lax.psum((q_gain_part, k_gain_part), ("dp", "seq"))
    return (attn_out, query_grad, key_grad, value_grad, q_gain_grad, k_gain_grad)


def solution(mesh):
    return jax.shard_map(
        per_device,
        mesh=mesh,
        in_specs=(
            P(("dp", "seq"), None),
            P(("dp", "seq"), None),
            P(("dp", "seq"), None),
            P(),
            P(),
            P(("dp", "seq"), None),
            P("dp", None),
            P("dp", None),
        ),
        out_specs=(
            P(("dp", "seq"), None),
            P(("dp", "seq"), None),
            P(("dp", "seq"), None),
            P(("dp", "seq"), None),
            P(),
            P(),
        ),
        check_vma=False,
    )
```

profile of v0, /device:TPU:0, one launch (start us, length us, event | category | flops | bytes accessed | tf_op | source)
XLA Modules:
  0.0 164.4 jit_solution(12461290162924541765)
XLA Ops:
  0.6 0.0 copy-start.1
  0.6 0.0 copy-start.5
  0.7 0.0 copy-start.2
  0.7 1.3 fusion.31
  2.0 1.2 fusion.33
  3.2 0.0 copy-start.3
  3.2 0.8 copy.112
  4.1 4.3 %all-to-all-start = ((bf16[128,4,512]{2,0,1:T(8,128)(2,1)}), bf16[128,4,512]{2,0,1:T(8,128)(2,1)S(1)}, u32[]{:S(2)}, u32[]{:S(2)}) async-start(bf16[128,4,512]{2,0,1:T(8,128)(2,1)} %bitcast.48), calls=%async_computation | async-start | bytes 1048576 | tf_op jit(solution)/shard_map/all_to_all | solution.py:100
  8.4 1.3 fusion.40
  9.6 0.0 copy-done.5
  9.6 0.2 fusion.42
  9.8 0.8 copy.111
  10.7 6.5 %all-to-all-done = bf16[128,4,512]{2,0,1:T(8,128)(2,1)S(1)} async-done(((bf16[128,4,512]{2,0,1:T(8,128)(2,1)}), bf16[128,4,512]{2,0,1:T(8,128)(2,1)S(1)}, u32[]{:S(2)}, u32[]{:S(2)}) %all-to-all-start) | async-done | bytes 524320 | tf_op jit(solution)/shard_map/all_to_all | solution.py:100
  17.2 3.5 %all-to-all-start.1 = ((bf16[128,4,512]{2,0,1:T(8,128)(2,1)}), bf16[128,4,512]{2,0,1:T(8,128)(2,1)S(1)}, u32[]{:S(2)}, u32[]{:S(2)}) async-start(bf16[128,4,512]{2,0,1:T(8,128)(2,1)} %bitcast.47), calls=%async_computation.1 | async-start | bytes 1048576 | tf_op jit(solution)/shard_map/all_to_all | solution.py:101
  20.7 0.8 copy.110
  21.5 7.9 %all-to-all-done.1 = bf16[128,4,512]{2,0,1:T(8,128)(2,1)S(1)} async-done(((bf16[128,4,512]{2,0,1:T(8,128)(2,1)}), bf16[128,4,512]{2,0,1:T(8,128)(2,1)S(1)}, u32[]{:S(2)}, u32[]{:S(2)}) %all-to-all-start.1) | async-done | bytes 524320 | tf_op jit(solution)/shard_map/all_to_all | solution.py:101
  29.4 3.5 %all-to-all-start.2 = ((bf16[128,4,512]{2,0,1:T(8,128)(2,1)}), bf16[128,4,512]{2,0,1:T(8,128)(2,1)S(1)}, u32[]{:S(2)}, u32[]{:S(2)}) async-start(bf16[128,4,512]{2,0,1:T(8,128)(2,1)} %bitcast.46), calls=%async_computation.2 | async-start | bytes 1048576 | tf_op jit(solution)/shard_map/all_to_all | solution.py:102
  32.9 0.8 copy.109
  33.8 7.9 %all-to-all-done.2 = bf16[128,4,512]{2,0,1:T(8,128)(2,1)S(1)} async-done(((bf16[128,4,512]{2,0,1:T(8,128)(2,1)}), bf16[128,4,512]{2,0,1:T(8,128)(2,1)S(1)}, u32[]{:S(2)}, u32[]{:S(2)}) %all-to-all-start.2) | async-done | bytes 524320 | tf_op jit(solution)/shard_map/all_to_all | solution.py:102
  41.7 3.5 %all-to-all-start.4 = ((bf16[128,4,512]{2,0,1:T(8,128)(2,1)}), bf16[128,4,512]{2,0,1:T(8,128)(2,1)S(1)}, u32[]{:S(2)}, u32[]{:S(2)}) async-start(bf16[128,4,512]{2,0,1:T(8,128)(2,1)} %bitcast.45), calls=%async_computation.4 | async-start | bytes 1048576 | tf_op jit(solution)/shard_map/all_to_all | solution.py:106
  45.2 0.3 fusion.52
  45.5 0.1 reshape.189
  45.6 1.1 copy.79
  46.7 0.1 reshape.190
  46.9 0.3 copy.75
  47.2 0.1 reshape.191
  47.3 6.6 %all-to-all-done.4 = bf16[128,4,512]{2,0,1:T(8,128)(2,1)S(1)} async-done(((bf16[128,4,512]{2,0,1:T(8,128)(2,1)}), bf16[128,4,512]{2,0,1:T(8,128)(2,1)S(1)}, u32[]{:S(2)}, u32[]{:S(2)}) %all-to-all-start.4) | async-done | bytes 524320 | tf_op jit(solution)/shard_map/all_to_all | solution.py:106
  53.9 0.1 reshape.192
  54.1 4.7 %fusion.66 = (f32[4,512]{1,0:T(4,128)S(1)}, f32[4,512,512]{1,2,0:T(8,128)}) fusion(pred[512,512]{0,1:T(8,128)(4,1)S(1)} %fusion.52, bf16[512,4,128]{0,2,1:T(8,128)(2,1)} %copy.79, bf16[512,4,128]{0,2,1:T(8,128)(2,1)S(1)} %copy.75), kind=kOutput, calls=%fused_computation.80 | convolution fusion | flops 272630272 | bytes 5513216 | tf_op jit(solution)/shard_map/while/body/eval_jaxpr/sub | solution.py:52
  58.7 2.9 %fusion.30 = bf16[512,4,128]{2,0,1:T(8,128)(2,1)S(1)} fusion(bf16[512,4,128]{2,1,0:T(4,128)(2,1)S(1)} %reshape.192, f32[4,512,512]{1,2,0:T(8,128)} %get-tuple-element.92, f32[4,512]{1,0:T(4,128)S(1)} %get-tuple-element.91), kind=kOutput, calls=%fused_computation.33 | convolution fusion | flops 270794752 | bytes 5251072 | tf_op jit(solution)/shard_map/while/body/eval_jaxpr/hst,shd->thd/dot_general | solution.py:68
  61.7 0.4 copy.84
  62.1 1.0 convert_element_type.117
  63.1 3.5 %all-to-all-start.7 = ((bf16[4,128,512]{2,1,0:T(8,128)(2,1)}), bf16[4,128,512]{2,1,0:T(8,128)(2,1)S(1)}, u32[]{:S(2)}, u32[]{:S(2)}) async-start(bf16[4,128,512]{2,1,0:T(8,128)(2,1)} %convert_element_type.117), calls=%async_computation.7 | async-start | bytes 1048576 | tf_op jit(solution)/shard_map/all_to_all | solution.py:113
  66.5 3.1 %fusion.29 = bf16[512,4,128]{2,0,1:T(8,128)(2,1)S(1)} fusion(bf16[512,4,128]{2,1,0:T(4,128)(2,1)S(1)} %reshape.191, f32[4,512,512]{1,2,0:T(8,128)} %get-tuple-element.92, f32[4,512]{1,0:T(4,128)S(1)} %get-tuple-element.91), kind=kOutput, calls=%fused_computation.32 | convolution fusion | flops 270794752 | bytes 5251072 | tf_op jit(solution)/shard_map/while/body/eval_jaxpr/hst,thd->shd/dot_general | solution.py:58
  69.6 0.4 copy.70
  70.1 1.0 convert_element_type.99
  71.1 4.3 %all-to-all-done.7 = bf16[4,128,512]{2,1,0:T(8,128)(2,1)S(1)} async-done(((bf16[4,128,512]{2,1,0:T(8,128)(2,1)}), bf16[4,128,512]{2,1,0:T(8,128)(2,1)S(1)}, u32[]{:S(2)}, u32[]{:S(2)}) %all-to-all-start.7) | async-done | bytes 524320 | tf_op jit(solution)/shard_map/all_to_all | solution.py:113
  75.3 3.5 %all-to-all-start.3 = ((bf16[4,128,512]{2,1,0:T(8,128)(2,1)}), bf16[4,128,512]{2,1,0:T(8,128)(2,1)S(1)}, u32[]{:S(2)}, u32[]{:S(2)}) async-start(bf16[4,128,512]{2,1,0:T(8,128)(2,1)} %convert_element_type.99), calls=%async_computation.3 | async-start | bytes 1048576 | tf_op jit(solution)/shard_map/all_to_all | solution.py:105
  78.8 2.7 %fusion.54 = f32[4,512,512]{1,2,0:T(8,128)} fusion(bf16[512,4,128]{2,1,0:T(4,128)(2,1)S(1)} %reshape.192, bf16[512,4,128]{2,1,0:T(4,128)(2,1)S(1)} %reshape.191), kind=kOutput, calls=%fused_computation.62 | convolution fusion | flops 268435456 | bytes 5242880 | tf_op jit(solution)/shard_map/while/body/eval_jaxpr/shd,thd->hst/dot_general | solution.py:67
  81.5 7.6 %fusion.23 = bf16[512,4,128]{0,2,1:T(8,128)(2,1)S(1)} fusion(bf16[512,4,128]{0,2,1:T(8,128)(2,1)} %copy.79, f32[4,512,512]{1,2,0:T(8,128)} %fusion.54, f32[4,512,512]{1,2,0:T(8,128)} %get-tuple-element.92, f32[4,512]{1,0:T(4,128)S(1)} %get-tuple-element.91), kind=kOutput, calls=%fused_computation.30 | convolution fusion | flops 276040192 | bytes 9445376 | tf_op jit(solution)/shard_map/while/body/eval_jaxpr/hst,shd->thd/dot_general | solution.py:78
  89.1 0.1 convert_element_type.110
  89.2 0.9 copy.81
  90.1 0.0 all-to-all-done.3
  90.1 3.5 %all-to-all-start.6 = ((bf16[4,128,512]{1,2,0:T(8,128)(2,1)}), bf16[4,128,512]{1,2,0:T(8,128)(2,1)S(1)}, u32[]{:S(2)}, u32[]{:S(2)}) async-start(bf16[4,128,512]{1,2,0:T(8,128)(2,1)} %copy.81), calls=%async_computation.6 | async-start | bytes 1048576 | tf_op jit(solution)/shard_map/all_to_all | solution.py:112
  93.6 8.5 %fusion.26 = bf16[512,4,128]{0,2,1:T(8,128)(2,1)} fusion(bf16[512,4,128]{0,2,1:T(8,128)(2,1)S(1)} %copy.75, f32[4,512,512]{1,2,0:T(8,128)} %fusion.54, f32[4,512,512]{1,2,0:T(8,128)} %get-tuple-element.92, f32[4,512]{1,0:T(4,128)S(1)} %get-tuple-element.91), kind=kOutput, calls=%fused_computation.31 | convolution fusion | flops 276040192 | bytes 9445376 | tf_op jit(solution)/shard_map/while/body/eval_jaxpr/hst,thd->shd/dot_general | solution.py:74
  102.1 1.2 convert_element_type.103
  103.3 0.9 copy.77
  104.2 0.0 all-to-all-done.6
  104.2 4.3 %all-to-all-start.5 = ((bf16[4,128,512]{1,2,0:T(8,128)(2,1)}), bf16[4,128,512]{1,2,0:T(8,128)(2,1)}, u32[]{:S(2)}, u32[]{:S(2)}) async-start(bf16[4,128,512]{1,2,0:T(8,128)(2,1)} %copy.77), calls=%async_computation.5 | async-start | bytes 1048576 | tf_op jit(solution)/shard_map/all_to_all | solution.py:111
  108.5 0.3 copy.85
  108.8 1.0 copy.89
  109.8 0.3 copy.71
  110.0 0.0 copy-start
  110.1 0.0 copy-start.4
  110.1 1.0 copy.88
  111.1 0.1 convert_element_type.121
  111.2 0.3 copy.82
  111.5 5.8 %all-to-all-done.5 = bf16[4,128,512]{1,2,0:T(8,128)(2,1)} async-done(((bf16[4,128,512]{1,2,0:T(8,128)(2,1)}), bf16[4,128,512]{1,2,0:T(8,128)(2,1)}, u32[]{:S(2)}, u32[]{:S(2)}) %all-to-all-start.5) | async-done | bytes 524320 | tf_op jit(solution)/shard_map/all_to_all | solution.py:111
  117.3 2.1 %convert_element_type.120 = f32[4,128,512]{1,2,0:T(8,128)} convert(bf16[4,128,512]{1,2,0:T(8,128)(2,1)} %all-to-all-done.5) | non-fusion elementwise | flops 262144 | bytes 1572864 | tf_op jit(solution)/shard_map/convert_element_type | solution.py:18
  119.4 1.6 copy.78
  121.0 0.6 fusion.39
  121.7 40.3 %all-reduce = (f32[2048]{0:T(1024)}, f32[2048]{0:T(1024)}) all-reduce(f32[2048]{0:T(1024)S(1)} %get-tuple-element.71, f32[2048]{0:T(1024)S(1)} %get-tuple-element.94), channel_id=1, replica_groups=mesh['dp'=8,'seq'=4] {'dp','seq'}, use_global_device_ids=true, to_apply=%region_8.9 | all-reduce | flops 4096 | bytes 32768 | tf_op jit(solution)/shard_map/psum | solution.py:117
  162.0 1.2 fusion.36
  163.2 1.2 fusion.45
  (14 shorter events, 0.1 us)
Async XLA Ops:
  0.6 9.0 %copy-start.1 = (bf16[128,2048]{1,0:T(8,128)(2,1)S(1)}, bf16[128,2048]{1,0:T(8,128)(2,1)}, u32[]{:S(2)}) copy-start(bf16[128,2048]{1,0:T(8,128)(2,1)} %param.9) | copy-start | bytes 1572868
  0.6 9.0 %copy-start.5 = (f32[2048]{0:T(1024)S(1)}, f32[2048]{0:T(1024)}, u32[]{:S(2)}) copy-start(f32[2048]{0:T(1024)} %param.12) | copy-start | bytes 24580
  0.7 20.0 %copy-start.2 = (bf16[128,2048]{1,0:T(8,128)(2,1)S(1)}, bf16[128,2048]{1,0:T(8,128)(2,1)}, u32[]{:S(2)}) copy-start(bf16[128,2048]{1,0:T(8,128)(2,1)} %param.10) | copy-start | bytes 1572868
  3.2 29.7 %copy-start.3 = (bf16[128,2048]{1,0:T(8,128)(2,1)S(1)}, bf16[128,2048]{1,0:T(8,128)(2,1)}, u32[]{:S(2)}) copy-start(bf16[128,2048]{1,0:T(8,128)(2,1)} %param.13) | copy-start | bytes 1572868
  4.1 13.1 %all-to-all-start = ((bf16[128,4,512]{2,0,1:T(8,128)(2,1)}), bf16[128,4,512]{2,0,1:T(8,128)(2,1)S(1)}, u32[]{:S(2)}, u32[]{:S(2)}) async-start(bf16[128,4,512]{2,0,1:T(8,128)(2,1)} %bitcast.48), calls=%async_computation | async-start | bytes 1048576 | tf_op jit(solution)/shard_map/all_to_all | solution.py:100
  8.3 36.8 %copy-start.7 = (s32[1,512]{1,0:T(1,128)S(1)}, s32[1,512]{1,0:T(1,128)}, u32[]{:S(2)}) copy-start(s32[1,512]{1,0:T(1,128)} %param.15) | copy-start | bytes 6148
  8.3 36.8 %copy-start.6 = (s32[1,512]{1,0:T(1,128)S(1)}, s32[1,512]{1,0:T(1,128)}, u32[]{:S(2)}) copy-start(s32[1,512]{1,0:T(1,128)} %param.14) | copy-start | bytes 6148
  17.2 12.3 %all-to-all-start.1 = ((bf16[128,4,512]{2,0,1:T(8,128)(2,1)}), bf16[128,4,512]{2,0,1:T(8,128)(2,1)S(1)}, u32[]{:S(2)}, u32[]{:S(2)}) async-start(bf16[128,4,512]{2,0,1:T(8,128)(2,1)} %bitcast.47), calls=%async_computation.1 | async-start | bytes 1048576 | tf_op jit(solution)/shard_map/all_to_all | solution.py:101
  29.4 12.3 %all-to-all-start.2 = ((bf16[128,4,512]{2,0,1:T(8,128)(2,1)}), bf16[128,4,512]{2,0,1:T(8,128)(2,1)S(1)}, u32[]{:S(2)}, u32[]{:S(2)}) async-start(bf16[128,4,512]{2,0,1:T(8,128)(2,1)} %bitcast.46), calls=%async_computation.2 | async-start | bytes 1048576 | tf_op jit(solution)/shard_map/all_to_all | solution.py:102
  41.7 12.3 %all-to-all-start.4 = ((bf16[128,4,512]{2,0,1:T(8,128)(2,1)}), bf16[128,4,512]{2,0,1:T(8,128)(2,1)S(1)}, u32[]{:S(2)}, u32[]{:S(2)}) async-start(bf16[128,4,512]{2,0,1:T(8,128)(2,1)} %bitcast.45), calls=%async_computation.4 | async-start | bytes 1048576 | tf_op jit(solution)/shard_map/all_to_all | solution.py:106
  63.1 12.3 %all-to-all-start.7 = ((bf16[4,128,512]{2,1,0:T(8,128)(2,1)}), bf16[4,128,512]{2,1,0:T(8,128)(2,1)S(1)}, u32[]{:S(2)}, u32[]{:S(2)}) async-start(bf16[4,128,512]{2,1,0:T(8,128)(2,1)} %convert_element_type.117), calls=%async_computation.7 | async-start | bytes 1048576 | tf_op jit(solution)/shard_map/all_to_all | solution.py:113
  75.3 14.8 %all-to-all-start.3 = ((bf16[4,128,512]{2,1,0:T(8,128)(2,1)}), bf16[4,128,512]{2,1,0:T(8,128)(2,1)S(1)}, u32[]{:S(2)}, u32[]{:S(2)}) async-start(bf16[4,128,512]{2,1,0:T(8,128)(2,1)} %convert_element_type.99), calls=%async_computation.3 | async-start | bytes 1048576 | tf_op jit(solution)/shard_map/all_to_all | solution.py:105
  90.1 14.0 %all-to-all-start.6 = ((bf16[4,128,512]{1,2,0:T(8,128)(2,1)}), bf16[4,128,512]{1,2,0:T(8,128)(2,1)S(1)}, u32[]{:S(2)}, u32[]{:S(2)}) async-start(bf16[4,128,512]{1,2,0:T(8,128)(2,1)} %copy.81), calls=%async_computation.6 | async-start | bytes 1048576 | tf_op jit(solution)/shard_map/all_to_all | solution.py:112
  104.2 13.2 %all-to-all-start.5 = ((bf16[4,128,512]{1,2,0:T(8,128)(2,1)}), bf16[4,128,512]{1,2,0:T(8,128)(2,1)}, u32[]{:S(2)}, u32[]{:S(2)}) async-start(bf16[4,128,512]{1,2,0:T(8,128)(2,1)} %copy.77), calls=%async_computation.5 | async-start | bytes 1048576 | tf_op jit(solution)/shard_map/all_to_all | solution.py:111
  110.0 10.9 %copy-start = (bf16[128,2048]{1,0:T(8,128)(2,1)S(1)}, bf16[128,2048]{1,0:T(8,128)(2,1)}, u32[]{:S(2)}) copy-start(bf16[128,2048]{1,0:T(8,128)(2,1)} %param.8) | copy-start | bytes 1572868
  110.1 10.9 %copy-start.4 = (f32[2048]{0:T(1024)S(1)}, f32[2048]{0:T(1024)}, u32[]{:S(2)}) copy-start(f32[2048]{0:T(1024)} %param.11) | copy-start | bytes 24580
where the time goes:
time: 165 us; the launch traced here: 164 us
  blocking collectives  40.3 us (24%)
  waiting for transfers between devices  39.1 us (24%)
  matrix products  29.5 us (18%)
  starting transfers between devices  29.4 us (18%)
  local copies, waits for them, and re-layouts  15.6 us (9%)
  other arithmetic  9.54 us (6%)
    psum x1, blocking collectives, per_device(): lax.psum((q_gain_part, k_gain_part), ('dp', 'seq'))  40.3 us
    dot_general x1, matrix products, one_block(): jnp.einsum('hst,thd->shd', score_grad, k_three, preferred_element_type=jn...  8.53 us
    all_to_all x1, waiting for transfers between devices, per_device(): lax.all_to_all(k_norm, 'seq', split_axis=1, concat_axis=0, tiled=True)  7.93 us
    all_to_all x1, waiting for transfers between devices, per_device(): lax.all_to_all(values, 'seq', split_axis=1, concat_axis=0, tiled=True)  7.93 us
    dot_general x1, matrix products, one_block(): jnp.einsum('hst,shd->thd', score_grad, q_block, preferred_element_type=jn...  7.62 us
    all_to_all x1, waiting for transfers between devices, per_device(): lax.all_to_all(out_grad, 'seq', split_axis=1, concat_axis=0, tiled=True)  6.63 us
    all_to_all x1, waiting for transfers between devices, per_device(): lax.all_to_all(q_norm, 'seq', split_axis=1, concat_axis=0, tiled=True)  6.49 us
    all_to_all x1, waiting for transfers between devices, per_device(): lax.all_to_all(q_part, 'seq', split_axis=0, concat_axis=1, tiled=True)  5.84 us
  transfers between devices with their start and end apart: 8, of which 6 were waited for; matrix products, arithmetic and copies ran while one was open for 22% of the time, Pallas kernels for 0%

commit v1 on v0

--- a/solution.py
+++ b/solution.py
@@ -114,7 +114,13 @@
     )
     query_grad, q_gain_part = norm_back(queries, q_inv, q_gain, q_grad)
     key_grad, k_gain_part = norm_back(keys, k_inv, k_gain, k_grad)
-    q_gain_grad, k_gain_grad = lax.psum((q_gain_part, k_gain_part), ("dp", "seq"))
+
+    def page_keep_up(inp, axis_tag, link_axis):
+        for u in (axis_tag, link_axis):
+            inp = lax.psum(inp, axis_name=u)
+        return inp
+
+    q_gain_grad, k_gain_grad = page_keep_up((q_gain_part, k_gain_part), "seq", "dp")
     return (attn_out, query_grad, key_grad, value_grad, q_gain_grad, k_gain_grad)
 
 

time: 165 us -> 174 us (1.055)
  blocking collectives: 40.3 us -> 48.7 us
    psum x1 -> x2, blocking collectives: 40.3 us -> 48.7 us  [page_keep_up(): inp = lax.psum(inp, axis_name=u)]
  transfers between devices with their start and end apart: 8 -> 8, of which waited for: 6 -> 6; matrix products, arithmetic and copies ran while one was open for 22% -> 20% of each run, Pallas kernels for 0% -> 0%
where the time goes in v1:
time: 174 us; the launch traced here: 173 us
  blocking collectives  48.7 us (28%)
  waiting for transfers between devices  39.1 us (22%)
  matrix products  29.5 us (17%)
  starting transfers between devices  29.4 us (17%)
  local copies, waits for them, and re-layouts  15.6 us (9%)
  other arithmetic  9.53 us (5%)
    psum x2, blocking collectives, page_keep_up(): inp = lax.psum(inp, axis_name=u)  48.7 us
    dot_general x1, matrix products, one_block(): jnp.einsum('hst,thd->shd', score_grad, k_three, preferred_element_type=jn...  8.53 us
    all_to_all x1, waiting for transfers between devices, per_device(): lax.all_to_all(k_norm, 'seq', split_axis=1, concat_axis=0, tiled=True)  7.93 us
    all_to_all x1, waiting for transfers between devices, per_device(): lax.all_to_all(values, 'seq', split_axis=1, concat_axis=0, tiled=True)  7.93 us
    dot_general x1, matrix products, one_block(): jnp.einsum('hst,shd->thd', score_grad, q_block, preferred_element_type=jn...  7.62 us
    all_to_all x1, waiting for transfers between devices, per_device(): lax.all_to_all(out_grad, 'seq', split_axis=1, concat_axis=0, tiled=True)  6.63 us
    all_to_all x1, waiting for transfers between devices, per_device(): lax.all_to_all(q_norm, 'seq', split_axis=1, concat_axis=0, tiled=True)  6.49 us
    all_to_all x1, waiting for transfers between devices, per_device(): lax.all_to_all(q_part, 'seq', split_axis=0, concat_axis=1, tiled=True)  5.84 us
  transfers between devices with their start and end apart: 8, of which 6 were waited for; matrix products, arithmetic and copies ran while one was open for 20% of the time, Pallas kernels for 0%

profile of v1, /device:TPU:0, one launch (start us, length us, event | category | flops | bytes accessed | tf_op | source)
XLA Modules:
  0.0 172.8 jit_solution(4605501888853644709)
XLA Ops:
  0.6 0.0 copy-start.1
  0.6 0.0 copy-start.5
  0.7 0.0 copy-start.2
  0.7 1.3 fusion.31
  2.0 1.2 fusion.33
  3.2 0.0 copy-start.3
  3.2 0.8 copy.112
  4.1 4.3 %all-to-all-start = ((bf16[128,4,512]{2,0,1:T(8,128)(2,1)}), bf16[128,4,512]{2,0,1:T(8,128)(2,1)S(1)}, u32[]{:S(2)}, u32[]{:S(2)}) async-start(bf16[128,4,512]{2,0,1:T(8,128)(2,1)} %bitcast.48), calls=%async_computation | async-start | bytes 1048576 | tf_op jit(solution)/shard_map/all_to_all | solution.py:100
  8.4 1.3 fusion.40
  9.6 0.2 fusion.42
  9.8 0.8 copy.111
  10.7 6.5 %all-to-all-done = bf16[128,4,512]{2,0,1:T(8,128)(2,1)S(1)} async-done(((bf16[128,4,512]{2,0,1:T(8,128)(2,1)}), bf16[128,4,512]{2,0,1:T(8,128)(2,1)S(1)}, u32[]{:S(2)}, u32[]{:S(2)}) %all-to-all-start) | async-done | bytes 524320 | tf_op jit(solution)/shard_map/all_to_all | solution.py:100
  17.2 3.5 %all-to-all-start.1 = ((bf16[128,4,512]{2,0,1:T(8,128)(2,1)}), bf16[128,4,512]{2,0,1:T(8,128)(2,1)S(1)}, u32[]{:S(2)}, u32[]{:S(2)}) async-start(bf16[128,4,512]{2,0,1:T(8,128)(2,1)} %bitcast.47), calls=%async_computation.1 | async-start | bytes 1048576 | tf_op jit(solution)/shard_map/all_to_all | solution.py:101
  20.7 0.8 copy.110
  21.5 7.9 %all-to-all-done.1 = bf16[128,4,512]{2,0,1:T(8,128)(2,1)S(1)} async-done(((bf16[128,4,512]{2,0,1:T(8,128)(2,1)}), bf16[128,4,512]{2,0,1:T(8,128)(2,1)S(1)}, u32[]{:S(2)}, u32[]{:S(2)}) %all-to-all-start.1) | async-done | bytes 524320 | tf_op jit(solution)/shard_map/all_to_all | solution.py:101
  29.4 3.5 %all-to-all-start.2 = ((bf16[128,4,512]{2,0,1:T(8,128)(2,1)}), bf16[128,4,512]{2,0,1:T(8,128)(2,1)S(1)}, u32[]{:S(2)}, u32[]{:S(2)}) async-start(bf16[128,4,512]{2,0,1:T(8,128)(2,1)} %bitcast.46), calls=%async_computation.2 | async-start | bytes 1048576 | tf_op jit(solution)/shard_map/all_to_all | solution.py:102
  32.9 0.8 copy.109
  33.8 7.9 %all-to-all-done.2 = bf16[128,4,512]{2,0,1:T(8,128)(2,1)S(1)} async-done(((bf16[128,4,512]{2,0,1:T(8,128)(2,1)}), bf16[128,4,512]{2,0,1:T(8,128)(2,1)S(1)}, u32[]{:S(2)}, u32[]{:S(2)}) %all-to-all-start.2) | async-done | bytes 524320 | tf_op jit(solution)/shard_map/all_to_all | solution.py:102
  41.7 3.5 %all-to-all-start.4 = ((bf16[128,4,512]{2,0,1:T(8,128)(2,1)}), bf16[128,4,512]{2,0,1:T(8,128)(2,1)S(1)}, u32[]{:S(2)}, u32[]{:S(2)}) async-start(bf16[128,4,512]{2,0,1:T(8,128)(2,1)} %bitcast.45), calls=%async_computation.4 | async-start | bytes 1048576 | tf_op jit(solution)/shard_map/all_to_all | solution.py:106
  45.2 0.3 fusion.52
  45.5 0.1 reshape.189
  45.6 1.1 copy.79
  46.7 0.1 reshape.190
  46.9 0.3 copy.75
  47.2 0.1 reshape.191
  47.3 6.6 %all-to-all-done.4 = bf16[128,4,512]{2,0,1:T(8,128)(2,1)S(1)} async-done(((bf16[128,4,512]{2,0,1:T(8,128)(2,1)}), bf16[128,4,512]{2,0,1:T(8,128)(2,1)S(1)}, u32[]{:S(2)}, u32[]{:S(2)}) %all-to-all-start.4) | async-done | bytes 524320 | tf_op jit(solution)/shard_map/all_to_all | solution.py:106
  53.9 0.1 reshape.192
  54.1 4.7 %fusion.66 = (f32[4,512]{1,0:T(4,128)S(1)}, f32[4,512,512]{1,2,0:T(8,128)}) fusion(pred[512,512]{0,1:T(8,128)(4,1)S(1)} %fusion.52, bf16[512,4,128]{0,2,1:T(8,128)(2,1)} %copy.79, bf16[512,4,128]{0,2,1:T(8,128)(2,1)S(1)} %copy.75), kind=kOutput, calls=%fused_computation.80 | convolution fusion | flops 272630272 | bytes 5513216 | tf_op jit(solution)/shard_map/while/body/eval_jaxpr/sub | solution.py:52
  58.7 2.9 %fusion.30 = bf16[512,4,128]{2,0,1:T(8,128)(2,1)S(1)} fusion(bf16[512,4,128]{2,1,0:T(4,128)(2,1)S(1)} %reshape.192, f32[4,512,512]{1,2,0:T(8,128)} %get-tuple-element.94, f32[4,512]{1,0:T(4,128)S(1)} %get-tuple-element.93), kind=kOutput, calls=%fused_computation.33 | convolution fusion | flops 270794752 | bytes 5251072 | tf_op jit(solution)/shard_map/while/body/eval_jaxpr/hst,shd->thd/dot_general | solution.py:68
  61.7 0.4 copy.84
  62.1 1.0 convert_element_type.117
  63.1 3.5 %all-to-all-start.7 = ((bf16[4,128,512]{2,1,0:T(8,128)(2,1)}), bf16[4,128,512]{2,1,0:T(8,128)(2,1)S(1)}, u32[]{:S(2)}, u32[]{:S(2)}) async-start(bf16[4,128,512]{2,1,0:T(8,128)(2,1)} %convert_element_type.117), calls=%async_computation.7 | async-start | bytes 1048576 | tf_op jit(solution)/shard_map/all_to_all | solution.py:113
  66.5 3.1 %fusion.29 = bf16[512,4,128]{2,0,1:T(8,128)(2,1)S(1)} fusion(bf16[512,4,128]{2,1,0:T(4,128)(2,1)S(1)} %reshape.191, f32[4,512,512]{1,2,0:T(8,128)} %get-tuple-element.94, f32[4,512]{1,0:T(4,128)S(1)} %get-tuple-element.93), kind=kOutput, calls=%fused_computation.32 | convolution fusion | flops 270794752 | bytes 5251072 | tf_op jit(solution)/shard_map/while/body/eval_jaxpr/hst,thd->shd/dot_general | solution.py:58
  69.6 0.4 copy.70
  70.1 1.0 convert_element_type.99
  71.1 4.3 %all-to-all-done.7 = bf16[4,128,512]{2,1,0:T(8,128)(2,1)S(1)} async-done(((bf16[4,128,512]{2,1,0:T(8,128)(2,1)}), bf16[4,128,512]{2,1,0:T(8,128)(2,1)S(1)}, u32[]{:S(2)}, u32[]{:S(2)}) %all-to-all-start.7) | async-done | bytes 524320 | tf_op jit(solution)/shard_map/all_to_all | solution.py:113
  75.3 3.5 %all-to-all-start.3 = ((bf16[4,128,512]{2,1,0:T(8,128)(2,1)}), bf16[4,128,512]{2,1,0:T(8,128)(2,1)S(1)}, u32[]{:S(2)}, u32[]{:S(2)}) async-start(bf16[4,128,512]{2,1,0:T(8,128)(2,1)} %convert_element_type.99), calls=%async_computation.3 | async-start | bytes 1048576 | tf_op jit(solution)/shard_map/all_to_all | solution.py:105
  78.8 2.7 %fusion.54 = f32[4,512,512]{1,2,0:T(8,128)} fusion(bf16[512,4,128]{2,1,0:T(4,128)(2,1)S(1)} %reshape.192, bf16[512,4,128]{2,1,0:T(4,128)(2,1)S(1)} %reshape.191), kind=kOutput, calls=%fused_computation.62 | convolution fusion | flops 268435456 | bytes 5242880 | tf_op jit(solution)/shard_map/while/body/eval_jaxpr/shd,thd->hst/dot_general | solution.py:67
  81.5 7.6 %fusion.23 = bf16[512,4,128]{0,2,1:T(8,128)(2,1)S(1)} fusion(bf16[512,4,128]{0,2,1:T(8,128)(2,1)} %copy.79, f32[4,512,512]{1,2,0:T(8,128)} %fusion.54, f32[4,512,512]{1,2,0:T(8,128)} %get-tuple-element.94, f32[4,512]{1,0:T(4,128)S(1)} %get-tuple-element.93), kind=kOutput, calls=%fused_computation.30 | convolution fusion | flops 276040192 | bytes 9445376 | tf_op jit(solution)/shard_map/while/body/eval_jaxpr/hst,shd->thd/dot_general | solution.py:78
  89.1 0.1 convert_element_type.110
  89.2 0.9 copy.81
  90.1 0.0 all-to-all-done.3
  90.1 3.5 %all-to-all-start.6 = ((bf16[4,128,512]{1,2,0:T(8,128)(2,1)}), bf16[4,128,512]{1,2,0:T(8,128)(2,1)S(1)}, u32[]{:S(2)}, u32[]{:S(2)}) async-start(bf16[4,128,512]{1,2,0:T(8,128)(2,1)} %copy.81), calls=%async_computation.6 | async-start | bytes 1048576 | tf_op jit(solution)/shard_map/all_to_all | solution.py:112
  93.6 8.5 %fusion.26 = bf16[512,4,128]{0,2,1:T(8,128)(2,1)} fusion(bf16[512,4,128]{0,2,1:T(8,128)(2,1)S(1)} %copy.75, f32[4,512,512]{1,2,0:T(8,128)} %fusion.54, f32[4,512,512]{1,2,0:T(8,128)} %get-tuple-element.94, f32[4,512]{1,0:T(4,128)S(1)} %get-tuple-element.93), kind=kOutput, calls=%fused_computation.31 | convolution fusion | flops 276040192 | bytes 9445376 | tf_op jit(solution)/shard_map/while/body/eval_jaxpr/hst,thd->shd/dot_general | solution.py:74
  102.1 1.2 convert_element_type.103
  103.3 0.9 copy.77
  104.2 0.0 all-to-all-done.6
  104.2 4.3 %all-to-all-start.5 = ((bf16[4,128,512]{1,2,0:T(8,128)(2,1)}), bf16[4,128,512]{1,2,0:T(8,128)(2,1)}, u32[]{:S(2)}, u32[]{:S(2)}) async-start(bf16[4,128,512]{1,2,0:T(8,128)(2,1)} %copy.77), calls=%async_computation.5 | async-start | bytes 1048576 | tf_op jit(solution)/shard_map/all_to_all | solution.py:111
  108.5 0.3 copy.85
  108.8 1.0 copy.89
  109.8 0.3 copy.71
  110.0 0.0 copy-start
  110.1 0.0 copy-start.4
  110.1 1.0 copy.88
  111.1 0.1 convert_element_type.121
  111.2 0.3 copy.82
  111.5 5.8 %all-to-all-done.5 = bf16[4,128,512]{1,2,0:T(8,128)(2,1)} async-done(((bf16[4,128,512]{1,2,0:T(8,128)(2,1)}), bf16[4,128,512]{1,2,0:T(8,128)(2,1)}, u32[]{:S(2)}, u32[]{:S(2)}) %all-to-all-start.5) | async-done | bytes 524320 | tf_op jit(solution)/shard_map/all_to_all | solution.py:111
  117.3 2.1 %convert_element_type.120 = f32[4,128,512]{1,2,0:T(8,128)} convert(bf16[4,128,512]{1,2,0:T(8,128)(2,1)} %all-to-all-done.5) | non-fusion elementwise | flops 262144 | bytes 1572864 | tf_op jit(solution)/shard_map/convert_element_type | solution.py:18
  119.4 1.6 copy.78
  121.0 0.6 fusion.39
  121.7 10.1 %all-reduce.1 = (f32[2048]{0:T(1024)S(1)}, f32[2048]{0:T(1024)S(1)}) all-reduce(f32[2048]{0:T(1024)S(1)} %get-tuple-element.71, f32[2048]{0:T(1024)S(1)} %get-tuple-element.96), channel_id=1, replica_groups=mesh['dp'=8,'seq'=4] {'seq'}, use_global_device_ids=true, to_apply=%region_8.9 | all-reduce | flops 4096 | bytes 32768 | tf_op jit(solution)/shard_map/psum | solution.py:120
  131.8 38.6 %all-reduce = (f32[2048]{0:T(1024)}, f32[2048]{0:T(1024)}) all-reduce(f32[2048]{0:T(1024)S(1)} %get-tuple-element.87, f32[2048]{0:T(1024)S(1)} %get-tuple-element.88), channel_id=1, replica_groups=mesh['dp'=8,'seq'=4] {'dp'}, use_global_device_ids=true, to_apply=%region_9.10 | all-reduce | flops 4096 | bytes 32768 | tf_op jit(solution)/shard_map/psum | solution.py:120
  170.4 1.2 fusion.36
  171.6 1.2 fusion.45
  (15 shorter events, 0.1 us)
Async XLA Ops:
  0.6 9.0 %copy-start.1 = (bf16[128,2048]{1,0:T(8,128)(2,1)S(1)}, bf16[128,2048]{1,0:T(8,128)(2,1)}, u32[]{:S(2)}) copy-start(bf16[128,2048]{1,0:T(8,128)(2,1)} %param.9) | copy-start | bytes 1572868
  0.6 9.0 %copy-start.5 = (f32[2048]{0:T(1024)S(1)}, f32[2048]{0:T(1024)}, u32[]{:S(2)}) copy-start(f32[2048]{0:T(1024)} %param.12) | copy-start | bytes 24580
  0.7 20.0 %copy-start.2 = (bf16[128,2048]{1,0:T(8,128)(2,1)S(1)}, bf16[128,2048]{1,0:T(8,128)(2,1)}, u32[]{:S(2)}) copy-start(bf16[128,2048]{1,0:T(8,128)(2,1)} %param.10) | copy-start | bytes 1572868
  3.2 29.7 %copy-start.3 = (bf16[128,2048]{1,0:T(8,128)(2,1)S(1)}, bf16[128,2048]{1,0:T(8,128)(2,1)}, u32[]{:S(2)}) copy-start(bf16[128,2048]{1,0:T(8,128)(2,1)} %param.13) | copy-start | bytes 1572868
  4.1 13.1 %all-to-all-start = ((bf16[128,4,512]{2,0,1:T(8,128)(2,1)}), bf16[128,4,512]{2,0,1:T(8,128)(2,1)S(1)}, u32[]{:S(2)}, u32[]{:S(2)}) async-start(bf16[128,4,512]{2,0,1:T(8,128)(2,1)} %bitcast.48), calls=%async_computation | async-start | bytes 1048576 | tf_op jit(solution)/shard_map/all_to_all | solution.py:100
  8.3 36.8 %copy-start.7 = (s32[1,512]{1,0:T(1,128)S(1)}, s32[1,512]{1,0:T(1,128)}, u32[]{:S(2)}) copy-start(s32[1,512]{1,0:T(1,128)} %param.15) | copy-start | bytes 6148
  8.3 36.8 %copy-start.6 = (s32[1,512]{1,0:T(1,128)S(1)}, s32[1,512]{1,0:T(1,128)}, u32[]{:S(2)}) copy-start(s32[1,512]{1,0:T(1,128)} %param.14) | copy-start | bytes 6148
  17.2 12.3 %all-to-all-start.1 = ((bf16[128,4,512]{2,0,1:T(8,128)(2,1)}), bf16[128,4,512]{2,0,1:T(8,128)(2,1)S(1)}, u32[]{:S(2)}, u32[]{:S(2)}) async-start(bf16[128,4,512]{2,0,1:T(8,128)(2,1)} %bitcast.47), calls=%async_computation.1 | async-start | bytes 1048576 | tf_op jit(solution)/shard_map/all_to_all | solution.py:101
  29.4 12.3 %all-to-all-start.2 = ((bf16[128,4,512]{2,0,1:T(8,128)(2,1)}), bf16[128,4,512]{2,0,1:T(8,128)(2,1)S(1)}, u32[]{:S(2)}, u32[]{:S(2)}) async-start(bf16[128,4,512]{2,0,1:T(8,128)(2,1)} %bitcast.46), calls=%async_computation.2 | async-start | bytes 1048576 | tf_op jit(solution)/shard_map/all_to_all | solution.py:102
  41.7 12.3 %all-to-all-start.4 = ((bf16[128,4,512]{2,0,1:T(8,128)(2,1)}), bf16[128,4,512]{2,0,1:T(8,128)(2,1)S(1)}, u32[]{:S(2)}, u32[]{:S(2)}) async-start(bf16[128,4,512]{2,0,1:T(8,128)(2,1)} %bitcast.45), calls=%async_computation.4 | async-start | bytes 1048576 | tf_op jit(solution)/shard_map/all_to_all | solution.py:106
  63.1 12.3 %all-to-all-start.7 = ((bf16[4,128,512]{2,1,0:T(8,128)(2,1)}), bf16[4,128,512]{2,1,0:T(8,128)(2,1)S(1)}, u32[]{:S(2)}, u32[]{:S(2)}) async-start(bf16[4,128,512]{2,1,0:T(8,128)(2,1)} %convert_element_type.117), calls=%async_computation.7 | async-start | bytes 1048576 | tf_op jit(solution)/shard_map/all_to_all | solution.py:113
  75.3 14.8 %all-to-all-start.3 = ((bf16[4,128,512]{2,1,0:T(8,128)(2,1)}), bf16[4,128,512]{2,1,0:T(8,128)(2,1)S(1)}, u32[]{:S(2)}, u32[]{:S(2)}) async-start(bf16[4,128,512]{2,1,0:T(8,128)(2,1)} %convert_element_type.99), calls=%async_computation.3 | async-start | bytes 1048576 | tf_op jit(solution)/shard_map/all_to_all | solution.py:105
  90.1 14.0 %all-to-all-start.6 = ((bf16[4,128,512]{1,2,0:T(8,128)(2,1)}), bf16[4,128,512]{1,2,0:T(8,128)(2,1)S(1)}, u32[]{:S(2)}, u32[]{:S(2)}) async-start(bf16[4,128,512]{1,2,0:T(8,128)(2,1)} %copy.81), calls=%async_computation.6 | async-start | bytes 1048576 | tf_op jit(solution)/shard_map/all_to_all | solution.py:112
  104.2 13.2 %all-to-all-start.5 = ((bf16[4,128,512]{1,2,0:T(8,128)(2,1)}), bf16[4,128,512]{1,2,0:T(8,128)(2,1)}, u32[]{:S(2)}, u32[]{:S(2)}) async-start(bf16[4,128,512]{1,2,0:T(8,128)(2,1)} %copy.77), calls=%async_computation.5 | async-start | bytes 1048576 | tf_op jit(solution)/shard_map/all_to_all | solution.py:111
  110.0 10.9 %copy-start = (bf16[128,2048]{1,0:T(8,128)(2,1)S(1)}, bf16[128,2048]{1,0:T(8,128)(2,1)}, u32[]{:S(2)}) copy-start(bf16[128,2048]{1,0:T(8,128)(2,1)} %param.8) | copy-start | bytes 1572868
  110.1 10.9 %copy-start.4 = (f32[2048]{0:T(1024)S(1)}, f32[2048]{0:T(1024)}, u32[]{:S(2)}) copy-start(f32[2048]{0:T(1024)} %param.11) | copy-start | bytes 24580
